TPU v7x, 32 devices: a whole 2x2x4 slice. The times are simulated.
32 devices in a mesh: dev: 16 (over z, y, x), rep: 2 (over core).
Axes of the slice: x: 2, y: 2, z: 4, core: 2. Of those that a mesh axis runs over, the one named last changes fastest.
Arguments:
- node_features: bfloat16 [1024, 2, 3136], P('dev', 'rep'), may hold values from -6 to 6
- src_node: int32 [16, 16, 2], P('dev'), may hold values from 0 to 63
- dst_node: int32 [16, 16, 2], P('dev'), may hold values from 0 to 63
- counts: int32 [16, 16], P('dev'), may hold values from 1 to 2, as said below
- rotation: bfloat16 [16, 16, 2, 235], P('dev'), may hold values from -2 to 2
- w_zero: bfloat16 [896, 2, 448], P(None, 'rep'), may hold values from -0.1875 to 0.1875
- w_one: bfloat16 [2, 768, 2, 384], P(None, None, 'rep'), may hold values from -0.15625 to 0.15625
- w_two: bfloat16 [2, 640, 2, 320], P(None, None, 'rep'), may hold values from -0.15625 to 0.15625
- norm_gain: float32 [2, 3136], P('rep'), may hold values from 0.5 to 1.5
Outputs:
- updated: bfloat16 [1024, 2, 3136], P('dev', 'rep')
Inputs may be any that keep to these rules, and one draw needn't show every extreme that they name: Slots i < counts[s, d] hold edges, the others padding; in every draw some destination device receives 2 edges from every source device.
All inputs are finite; a program needn't handle non-finite values.
Results may differ from a plain program's by a relative error of at most 0.0054.
Values may be sent and summed in bfloat16 or wider, within the bound.
A program may use at most 64 MiB of HBM per device.

v0:
```python
import math

import jax
import jax.numpy as jnp
from jax import lax
from jax.sharding import PartitionSpec as P


def for_sending(value):
    return jax.tree.map(lambda a: a.astype(jnp.bfloat16) if a.dtype == jnp.float32 else a, value)


def frame_slot(degree, order):
    if order == 0:
        return degree
    if order == 1:
        return 6 + degree
    if order == -1:
        return 12 + degree
    if order == 2:
        return 17 + degree
    return 22 + degree


def frame_tables():
    offsets = []
    places = []
    spot = 0
    for degree in range(7):
        reach = min(degree, 2)
        offsets.append(spot)
        spot += (2 * degree + 1) * (2 * reach + 1)
        places.append([frame_slot(degree, order) for order in range(-reach, reach + 1)])
    return (offsets, places)


def block_of(rotation, offsets, degree):
    reach = min(degree, 2)
    span = 2 * degree + 1
    height = 2 * reach + 1
    piece = rotation[:, offsets[degree] : offsets[degree] + height * span]
    return piece.reshape(rotation.shape[0], height, span).astype(jnp.float32)


def frame(coeffs, rotation):
    offsets, places = frame_tables()
    pieces = []
    for degree in range(7):
        matrix = block_of(rotation, offsets, degree)
        part = coeffs[:, degree * degree : degree * degree + 2 * degree + 1, :].astype(jnp.float32)
        pieces.append(jnp.sum(matrix[:, :, :, None] * part[:, None, :, :], axis=2))
    listing = sorted(
        (
            (places[degree][row], degree, row)
            for degree in range(7)
            for row in range(len(places[degree]))
        )
    )
    return jnp.concatenate(
        [pieces[degree][:, row : row + 1, :] for place, degree, row in listing], axis=1
    )


def unframe(framed, rotation):
    offsets, places = frame_tables()
    parts = []
    for degree in range(7):
        matrix = block_of(rotation, offsets, degree)
        chosen = jnp.concatenate(
            [framed[:, place : place + 1, :] for place in places[degree]], axis=1
        ).astype(jnp.float32)
        parts.append(jnp.sum(matrix[:, :, :, None] * chosen[:, :, None, :], axis=1))
    return jnp.concatenate(parts, axis=1)


def mix_orders(rotated, zero_mat, one_mats, two_mats):
    batch = rotated.shape[0]
    out_width = zero_mat.shape[1] // 7
    flat_zero = rotated[:, 0:7, :].reshape(batch, -1)
    result = [
        jnp.dot(flat_zero, zero_mat, preferred_element_type=jnp.float32).reshape(
            batch, 7, out_width
        )
    ]
    for first, count, mats in ((7, 6, one_mats), (19, 5, two_mats)):
        plus = rotated[:, first : first + count, :].reshape(batch, -1)
        minus = rotated[:, first + count : first + 2 * count, :].reshape(batch, -1)
        upper = jnp.dot(plus, mats[0], preferred_element_type=jnp.float32) - jnp.dot(
            minus, mats[1], preferred_element_type=jnp.float32
        )
        lower = jnp.dot(plus, mats[1], preferred_element_type=jnp.float32) + jnp.dot(
            minus, mats[0], preferred_element_type=jnp.float32
        )
        result.append(upper.reshape(batch, count, out_width))
        result.append(lower.reshape(batch, count, out_width))
    return jnp.concatenate(result, axis=1).astype(jnp.bfloat16)


def by_blocks(func, arrays, size):
    count = arrays[0].shape[0] // size
    shaped = tuple((member.reshape((count, size) + member.shape[1:]) for member in arrays))
    result = lax.map(lambda items: func(*items), shaped)
    return result.reshape((count * size,) + result.shape[2:])


def shards(node_features, src_node, dst_node, counts, rotation, w_zero, w_one, w_two, norm_gain):
    nodes = node_features.shape[0]
    flat = node_features.shape[2]
    half_width = flat // 49
    peers = src_node.shape[1]
    slots = src_node.shape[2]
    edges = peers * slots
    sources = src_node.reshape(edges)
    rot_rows = rotation.reshape(edges, 235)
    size = math.gcd(edges, 512)
    both = lax.all_gather(node_features, "rep", axis=1, tiled=True)
    width = both.shape[1] * half_width
    full = both.reshape(nodes, -1, 49, half_width).transpose(0, 2, 1, 3).reshape(nodes, 49, width)

    def turn_whole(index, rows):
        return frame(jnp.take(full, index, axis=0), rows).astype(jnp.bfloat16)

    rotated = by_blocks(turn_whole, (sources, rot_rows), size)
    zero_mat = w_zero.reshape(w_zero.shape[0], -1)
    one_mats = w_one.reshape(2, w_one.shape[1], -1)
    two_mats = w_two.reshape(2, w_two.shape[1], -1)
    live = (
        (jnp.arange(slots)[None, :] < counts.reshape(peers)[:, None])
        .reshape(edges)
        .astype(jnp.bfloat16)
    )

    def finish(block_rows, rows, alive):
        edge_out = mix_orders(block_rows, zero_mat, one_mats, two_mats)
        back = unframe(edge_out, rows).astype(jnp.bfloat16)
        return back * alive[:, None, None]

    outgoing = by_blocks(finish, (rotated, rot_rows, live), size).reshape(
        peers, slots, 49 * half_width
    )
    received = (
        lax.all_to_all(for_sending(outgoing), "dev", split_axis=0, concat_axis=0, tiled=True)
        .astype(outgoing.dtype)
        .reshape(edges, 49 * half_width)
    )
    targets = dst_node.reshape(edges)
    one_hot = (jnp.arange(nodes)[:, None] == targets[None, :]).astype(jnp.bfloat16)
    total = jnp.dot(one_hot, received, preferred_element_type=jnp.float32)
    partial_sq = jnp.sum(total * total, axis=1)
    summed_sq = lax.psum(partial_sq, "rep")
    mean_sq = summed_sq / (49 * half_width * lax.axis_size("rep"))
    normed = total * lax.rsqrt(mean_sq + 1e-06)[:, None]
    updated = node_features.reshape(nodes, flat).astype(jnp.float32) + norm_gain * normed
    return updated.astype(jnp.bfloat16).reshape(nodes, 1, flat)


def solution(mesh):
    return jax.shard_map(
        shards,
        mesh=mesh,
        in_specs=(
            P("dev", "rep", None),
            P("dev", None, None),
            P("dev", None, None),
            P("dev", None),
            P("dev", None, None, None),
            P(None, "rep", None),
            P(None, None, "rep", None),
            P(None, None, "rep", None),
            P("rep", None),
        ),
        out_specs=P("dev", "rep", None),
        check_vma=False,
    )
```

profile of v0, /device:TPU:0, one launch (start us, length us, event | category | flops | bytes accessed | tf_op | source)
XLA Modules:
  0.0 44.6 jit_solution(1610045401548665702)
XLA Ops:
  0.0 0.8 %copy.239 = s32[1,16,2]{2,1,0:T(8,128)S(1)} copy(s32[1,16,2]{1,2,0:T(2,128)} %param.10) | data formatting | bytes 256 | tf_op args[1]
  0.8 0.1 squeeze.42
  0.9 0.1 squeeze.41
  1.0 2.7 %all_gather.3 = bf16[64,2,3136]{2,0,1:T(8,128)(2,1)S(1)} all-gather(bf16[64,1,3136]{2,0,1:T(8,128)(2,1)} %param.9), channel_id=1, replica_groups=mesh['dev'=16,'rep'=2] {'rep'}, dimensions={1}, use_global_device_ids=true | all-gather | bytes 1204224 | tf_op jit(solution)/shard_map/all_gather | solution.py:116
  3.7 0.9 %reshape.441 = bf16[64,2,49,64]{3,2,0,1:T(8,128)(2,1)S(1)} reshape(bf16[64,2,3136]{2,0,1:T(8,128)(2,1)S(1)} %all_gather.3) | data formatting | bytes 1605632 | tf_op jit(solution)/shard_map/reshape | solution.py:118
  4.7 2.8 %copy.278 = bf16[64,49,2,64]{3,2,1,0:T(2,128)(2,1)} copy(bf16[64,49,2,64]{3,1,0,2:T(8,128)(2,1)S(1)} %bitcast.103) | data formatting | bytes 1605632 | tf_op jit(solution)/shard_map/reshape | solution.py:118
  7.5 3.3 %reshape.472 = bf16[64,49,128]{2,1,0:T(8,128)(2,1)S(1)} reshape(bf16[64,49,2,64]{3,2,1,0:T(2,128)(2,1)} %copy.278) | data formatting | bytes 1605632 | tf_op jit(solution)/shard_map/reshape | solution.py:118
  10.9 0.6 %gather_fusion = bf16[32,49,128]{2,1,0:T(8,128)(2,1)S(1)} fusion(bf16[64,49,128]{2,1,0:T(8,128)(2,1)S(1)} %reshape.472, s32[1024]{0:T(1024)S(1)} %pad_clamp_fusion), kind=kCustom, calls=%fused_computation | custom fusion | bytes 802944 | tf_op jit(solution)/shard_map/while/body/eval_jaxpr/jit(_take)/gather | solution.py:121
  11.6 0.1 copy_select_fusion
  11.7 0.1 slice.476
  11.9 0.1 slice.479
  12.0 0.1 slice.482
  12.1 0.1 slice.485
  12.2 0.1 slice.488
  12.3 0.1 copy.282
  12.4 0.1 copy.281
  12.5 0.1 copy.280
  12.6 0.1 constant_dynamic-update-slice_fusion.6
  12.7 0.1 copy.283
  12.8 0.1 copy.284
  12.9 0.1 copy.285
  13.0 0.1 copy.286
  13.2 0.2 multiply_reduce_fusion.10
  13.3 0.1 multiply_reduce_fusion.12
  13.5 0.2 multiply_reduce_fusion.8
  13.7 0.3 multiply_reduce_fusion.6
  14.0 0.3 multiply_reduce_fusion.3
  14.3 0.3 multiply_reduce_fusion.1
  14.7 0.2 fusion.9
  15.0 0.2 fusion.5
  15.2 0.2 fusion.20
  15.4 0.2 fusion.16
  15.7 0.2 fusion.2
  15.9 0.1 reshape.451
  16.1 0.6 %constant_dynamic-update-slice_fusion.53 = bf16[32,5,64]{2,0,1:T(8,128)(2,1)} fusion(bf16[32,1,64]{2,1,0:T(2,128)(2,1)S(1)} %get-tuple-element.61), kind=kLoop, calls=%fused_computation.100 | loop fusion | bytes 12288
  16.7 0.2 fusion
  16.9 0.1 reshape.447
  17.0 0.1 fusion.48
  17.2 0.1 reshape.471
  17.3 0.2 fusion.1
  17.5 0.1 reshape.448
  17.6 0.1 fusion.47
  17.7 0.6 %constant_dynamic-update-slice_fusion.52 = bf16[32,5,64]{2,0,1:T(8,128)(2,1)} fusion(bf16[32,5,64]{2,0,1:T(8,128)(2,1)} %constant_dynamic-update-slice_fusion.53, bf16[32,1,64]{2,1,0:T(2,128)(2,1)S(1)} %get-tuple-element.54), kind=kLoop, calls=%fused_computation.99 | loop fusion | bytes 12288
  18.3 0.5 %convolution_convert_fusion = bf16[32,7,64]{2,0,1:T(8,128)(2,1)S(1)} fusion(bf16[32,896,1]{1,0,2:T(8,128)(2,1)S(1)} %reshape.471, bf16[7,64,896]{2,1,0:T(8,128)(2,1)S(1)} %bitcast.102), kind=kOutput, calls=%fused_computation.1 | convolution fusion | flops 25704448 | bytes 888832 | tf_op jit(solution)/shard_map/while/body/eval_jaxpr/dot_general | solution.py:81
  18.9 0.6 %constant_dynamic-update-slice_fusion.51 = (bf16[32,5,64]{2,0,1:T(8,128)(2,1)}, bf16[32,5,64]{2,0,1:T(8,128)(2,1)S(1)}, bf16[32,5,64]{2,0,1:T(8,128)(2,1)S(1)}, ...) fusion(bf16[32,5,64]{2,0,1:T(8,128)(2,1)} %constant_dynamic-upd, ...), kind=kLoop, calls=%fused_computation.98 | loop fusion | flops 6143 | bytes 115200
  19.5 0.1 multiply_reduce_fusion.11
  19.7 0.2 fusion.3
  19.9 0.1 reshape.452
  20.1 0.2 multiply_reduce_fusion.9
  20.4 0.2 multiply_reduce_fusion.7
  20.6 0.3 multiply_reduce_fusion.5
  20.9 0.3 multiply_reduce_fusion.2
  21.3 0.3 multiply_reduce_fusion
  21.8 0.2 copy.277
  22.0 0.3 convert_element_type.227
  22.4 0.9 %broadcast_multiply_fusion = bf16[16,2,3136]{2,1,0:T(2,128)(2,1)} fusion(bf16[16,2,3136]{2,1,0:T(2,128)(2,1)S(1)} %convert_element_type.227, bf16[16,2]{1,0:T(8,128)(2,1)S(1)} %fusion.44), kind=kLoop, calls=%fused_computation.109 | loop fusion | flops 100352 | bytes 401472 | tf_op jit(solution)/shard_map/while/body/eval_jaxpr/mul | solution.py:136
  23.3 8.2 %all-to-all-start = ((bf16[16,2,3136]{2,1,0:T(2,128)(2,1)}), bf16[16,2,3136]{2,1,0:T(2,128)(2,1)S(1)}, u32[]{:S(2)}, u32[]{:S(2)}) async-start(bf16[16,2,3136]{2,1,0:T(2,128)(2,1)} %broadcast_multiply_fusion), calls=%async_computation | async-start | bytes 409600 | tf_op jit(solution)/shard_map/all_to_all | solution.py:142
  31.6 0.1 copy.237
  31.6 0.1 eq.16
  31.8 8.9 %all-to-all-done = bf16[16,2,3136]{2,1,0:T(2,128)(2,1)S(1)} async-done(((bf16[16,2,3136]{2,1,0:T(2,128)(2,1)}), bf16[16,2,3136]{2,1,0:T(2,128)(2,1)S(1)}, u32[]{:S(2)}, u32[]{:S(2)}) %all-to-all-start) | async-done | bytes 200736 | tf_op jit(solution)/shard_map/all_to_all | solution.py:142
  40.6 0.2 reshape.453
  40.8 0.3 multiply_reduce_fusion.4
  41.1 2.5 %psum.7 = f32[64]{0:T(128)S(1)} all-reduce(f32[64]{0:T(128)S(1)} %get-tuple-element.101), channel_id=1, replica_groups=mesh['dev'=16,'rep'=2] {'rep'}, use_global_device_ids=true, to_apply=%region_13.14 | all-reduce | flops 64 | bytes 512 | tf_op jit(solution)/shard_map/psum | solution.py:150
  43.6 0.9 %fusion.15 = bf16[64,1,3136]{2,0,1:T(8,128)(2,1)} fusion(f32[64,3136]{1,0:T(8,128)S(1)} %get-tuple-element.102, bf16[64,1,3136]{2,0,1:T(8,128)(2,1)S(1)} %copy-done.3, f32[64]{0:T(128)S(1)} %add_rsqrt_fusion, f32[3136]{0:T(1024)S(1)} %reduce), kind=kLoop, calls=%fused_computation.31 | loop fusion | flops 1003520 | bytes 1618432 | tf_op jit(solution)/shard_map/reshape | solution.py:154
  (83 shorter events, 1.0 us)
Async XLA Ops:
  0.0 18.3 %copy-start = (bf16[896,1,448]{0,2,1:T(8,128)(2,1)S(1)}, bf16[896,1,448]{0,2,1:T(8,128)(2,1)}, u32[]{:S(2)}) copy-start(bf16[896,1,448]{0,2,1:T(8,128)(2,1)} %param.14) | copy-start | bytes 2408452
  10.8 0.8 %copy-start.5 = (bf16[1,16,2,235]{3,2,1,0:T(2,128)(2,1)S(1)}, bf16[1,16,2,235]{3,2,1,0:T(2,128)(2,1)}, u32[]{:S(2)}) copy-start(bf16[1,16,2,235]{3,2,1,0:T(2,128)(2,1)} %param.13) | copy-start | bytes 45124
  12.2 2.6 %copy-start.1 = (bf16[2,768,1,384]{3,1,2,0:T(8,128)(2,1)S(1)}, bf16[2,768,1,384]{3,1,2,0:T(8,128)(2,1)}, u32[]{:S(2)}) copy-start(bf16[2,768,1,384]{3,1,2,0:T(8,128)(2,1)} %param.15) | copy-start | bytes 3538948
  12.6 1.1 %copy-start.7 = (f32[32]{0:T(128)}, f32[32]{0:T(128)S(1)}, u32[]{:S(2)}) copy-start(f32[32]{0:T(128)S(1)} %bitcast_convert_fusion) | copy-start | bytes 388
  14.0 1.2 %copy-start.2 = (bf16[2,640,1,320]{1,3,2,0:T(8,128)(2,1)S(1)}, bf16[2,640,1,320]{1,3,2,0:T(8,128)(2,1)}, u32[]{:S(2)}) copy-start(bf16[2,640,1,320]{1,3,2,0:T(8,128)(2,1)} %param.16) | copy-start | bytes 2457604
  17.2 1.8 %copy-start.8 = (f32[32]{0:T(128)S(1)}, f32[32]{0:T(128)}, u32[]{:S(2)}) copy-start(f32[32]{0:T(128)} %copy-done.7) | copy-start | bytes 388
  19.5 1.7 %copy-start.4 = (bf16[32,5,64]{2,0,1:T(8,128)(2,1)S(1)}, bf16[32,5,64]{2,0,1:T(8,128)(2,1)}, u32[]{:S(2)}) copy-start(bf16[32,5,64]{2,0,1:T(8,128)(2,1)} %get-tuple-element.66) | copy-start | bytes 61444
  21.6 0.7 %copy-start.10 = (s32[1,16]{1,0:T(1,128)S(1)}, s32[1,16]{1,0:T(1,128)}, u32[]{:S(2)}) copy-start(s32[1,16]{1,0:T(1,128)} %param.12) | copy-start | bytes 196
  21.8 9.8 %copy-start.9 = (s32[1,16,2]{1,2,0:T(2,128)S(1)}, s32[1,16,2]{1,2,0:T(2,128)}, u32[]{:S(2)}) copy-start(s32[1,16,2]{1,2,0:T(2,128)} %param.11) | copy-start | bytes 388
  21.8 9.9 %copy-start.6 = (f32[1,3136]{1,0:T(1,128)S(1)}, f32[1,3136]{1,0:T(1,128)}, u32[]{:S(2)}) copy-start(f32[1,3136]{1,0:T(1,128)} %param.17) | copy-start | bytes 37636
  22.3 21.4 %copy-start.3 = (bf16[64,1,3136]{2,0,1:T(8,128)(2,1)S(1)}, bf16[64,1,3136]{2,0,1:T(8,128)(2,1)}, u32[]{:S(2)}) copy-start(bf16[64,1,3136]{2,0,1:T(8,128)(2,1)} %param.9) | copy-start | bytes 1204228
  23.3 17.3 %all-to-all-start = ((bf16[16,2,3136]{2,1,0:T(2,128)(2,1)}), bf16[16,2,3136]{2,1,0:T(2,128)(2,1)S(1)}, u32[]{:S(2)}, u32[]{:S(2)}) async-start(bf16[16,2,3136]{2,1,0:T(2,128)(2,1)} %broadcast_multiply_fusion), calls=%async_computation | async-start | bytes 409600 | tf_op jit(solution)/shard_map/all_to_all | solution.py:142
where the time goes:
time: 44.9 us; the launch traced here: 44.6 us
  local copies, waits for them, and re-layouts  13.2 us (29%)
  waiting for transfers between devices  8.86 us (20%)
  starting transfers between devices  8.22 us (18%)
  other arithmetic  5.73 us (13%)
  blocking collectives  5.19 us (12%)
  matrix products  2.61 us (6%)
  between operations  0.73 us (2%)
    all_to_all x1, waiting for transfers between devices, shards(): lax.all_to_all(for_sending(outgoing), 'dev', split_axis=0, concat_axis=0,...  8.86 us
    all_to_all x1, starting transfers between devices, shards(): lax.all_to_all(for_sending(outgoing), 'dev', split_axis=0, concat_axis=0,...  8.22 us
    reshape x3, local copies, waits for them, and re-layouts, shards(): both.reshape(nodes, -1, 49, half_width).transpose(0, 2, 1, 3)  7.1 us
    unnamed x56, local copies, waits for them, and re-layouts  3.15 us
    all_gather x1, blocking collectives, shards(): both = lax.all_gather(node_features, 'rep', axis=1, tiled=True)  2.72 us
    psum x1, blocking collectives, shards(): summed_sq = lax.psum(partial_sq, 'rep')  2.47 us
    reduce_sum x6, other arithmetic, unframe(): parts.append(jnp.sum(matrix[:, :, :, None] * chosen[:, :, None, :], axis=1))  1.39 us
    reduce_sum x6, other arithmetic, frame(): pieces.append(jnp.sum(matrix[:, :, :, None] * part[:, None, :, :], axis=2))  1.39 us
  transfers between devices with their start and end apart: 1, of which 1 were waited for; matrix products, arithmetic and copies ran while one was open for 0% of the time, Pallas kernels for 0%

commit v1 on v0

v1 whole, which is shorter than its diff:
```python
import functools

import jax
import jax.numpy as jnp
from jax import lax
from jax.experimental import pallas as pl
from jax.experimental.pallas import tpu as pltpu
from jax.sharding import PartitionSpec as P

LANES = 128
HALF = 64
COEFFS = 49
FRAME = 29
ROT = 235
WINDOW = 120
TILES = (COEFFS + 1) // 2
WIDE = TILES * LANES
GROUPS = ((0, 7, 0), (7, 6, 512), (13, 6, 896), (19, 5, 1280), (24, 5, 1664))
MESSAGE = 2048
BLOCK = 32
MESH = pl.DeviceIdType.MESH


def frame_slot(degree, order):
    if order == 0:
        return degree
    if order == 1:
        return 6 + degree
    if order == -1:
        return 12 + degree
    if order == 2:
        return 17 + degree
    return 22 + degree


def terms():
    listing = []
    spot = 0
    for degree in range(7):
        reach = min(degree, 2)
        span = 2 * degree + 1
        first = degree * degree
        for row in range(2 * reach + 1):
            slot = frame_slot(degree, row - reach)
            for tile in range(first // 2, (first + span - 1) // 2 + 1):
                ends = []
                for coeff in (2 * tile, 2 * tile + 1):
                    inside = first <= coeff < first + span
                    ends.append(spot + row * span + coeff - first if inside else None)
                listing.append((slot, tile, ends[0], ends[1]))
        spot += span * (2 * reach + 1)
    return listing


TERMS = terms()


def message_place(slot):
    for first, count, base in GROUPS:
        if first <= slot < first + count:
            lane = base + (slot - first) * HALF
            return lane // LANES, (lane % LANES) // HALF
    raise ValueError


def each(count, func):
    if count <= 16:
        for index in range(count):
            func(index)
    else:
        lax.fori_loop(0, count, lambda index, carry: (func(index), carry)[1], 0)


def kernel(
    peers,
    slots,
    x_ref,
    src_ref,
    dst_ref,
    rot_ref,
    gain_ref,
    w0_hbm,
    w1_hbm,
    w2_hbm,
    out_ref,
    w0,
    w1,
    w2,
    low_scr,
    high_scr,
    xg,
    own,
    packed,
    other,
    lhs,
    y_scr,
    msg,
    recv,
    rrot,
    mult,
    f_scr,
    back,
    total,
    sq,
    sq_other,
    wsem,
    esem,
    rot_send,
    rot_recv,
    msg_send,
    msg_recv,
    qsem,
):
    me = lax.axis_index("dev")
    half = lax.axis_index("rep")
    nodes = x_ref.shape[0]
    flat = x_ref.shape[1]
    blocks = peers * slots // BLOCK
    group = BLOCK // slots
    partner = {"rep": 1 - half}

    def peer(offset):
        return lax.rem(me + offset, peers)

    weights = [
        pltpu.make_async_copy(src, dst, wsem.at[index])
        for index, (src, dst) in enumerate(((w0_hbm, w0), (w1_hbm, w1), (w2_hbm, w2)))
    ]
    barrier = pltpu.get_barrier_semaphore()
    pl.semaphore_signal(barrier, inc=1, device_id=partner, device_id_type=MESH)
    each(
        peers - 1,
        lambda o: pl.semaphore_signal(
            barrier, inc=1, device_id={"dev": peer(o + 1)}, device_id_type=MESH
        ),
    )
    for copy in weights:
        copy.start()

    lane = lax.broadcasted_iota(jnp.int32, (BLOCK, LANES), 1)
    low_half = lane < HALF
    mine = (lane // HALF) == half

    y_scr[...] = jnp.zeros_like(y_scr)
    xg[:, (TILES - 1) * LANES :] = jnp.zeros((BLOCK, LANES), jnp.float32)
    low_scr[...] = jnp.zeros_like(low_scr)
    high_scr[...] = jnp.zeros_like(high_scr)

    def load_rotation(ref, start):
        for index in range(group):
            rows = ref[start + index].astype(jnp.float32)
            low_scr[index * slots : (index + 1) * slots, 0:WINDOW] = rows[:, 0:WINDOW]
            high_scr[index * slots : (index + 1) * slots, 0:WINDOW] = rows[:, ROT - WINDOW :]
        return low_scr[...], high_scr[...]

    def multiplier(tables, first, second):
        given = [entry for entry in (first, second) if entry is not None]
        which = 0 if max(given) < WINDOW else 1
        shift = which * (ROT - WINDOW)
        places = [WINDOW if e is None else e - shift for e in (first, second)]
        index = jnp.where(low_half, places[0], places[1])
        return jnp.take_along_axis(tables[which], index, axis=1, mode="promise_in_bounds")

    def turn(block):
        tables = load_rotation(rot_ref, block * group)
        rows = pl.multiple_of(block * BLOCK, BLOCK)
        hot = (
            lax.broadcasted_iota(jnp.int32, (BLOCK, nodes), 1) == src_ref[pl.ds(rows, BLOCK), :]
        ).astype(jnp.bfloat16)
        xg[:, 0:flat] = jnp.dot(hot, x_ref[...], preferred_element_type=jnp.float32)
        sums = [None] * FRAME
        for slot, tile, first, second in TERMS:
            part = multiplier(tables, first, second) * xg[:, tile * LANES : (tile + 1) * LANES]
            sums[slot] = part if sums[slot] is None else sums[slot] + part
        for slot in range(FRAME):
            sums[slot] = sums[slot] + pltpu.roll(sums[slot], HALF, 1)
            own[block, :, slot * LANES : (slot + 1) * LANES] = sums[slot]
        for pair in range((FRAME + 1) // 2):
            first = sums[2 * pair]
            second = sums[min(2 * pair + 1, FRAME - 1)]
            packed[block, :, pair * LANES : (pair + 1) * LANES] = jnp.where(
                mine, first, second
            ).astype(jnp.bfloat16)

    each(blocks, turn)

    pl.semaphore_wait(barrier, peers)

    exchange = pltpu.make_async_remote_copy(
        src_ref=packed,
        dst_ref=other,
        send_sem=esem.at[0],
        recv_sem=esem.at[1],
        device_id=partner,
        device_id_type=MESH,
    )
    exchange.start()

    def transfer(source, target, send, receive, o, landing):
        to = peer(o + 1)
        spot = me if landing is None else landing
        return pltpu.make_async_remote_copy(
            src_ref=source.at[to],
            dst_ref=target.at[spot],
            send_sem=send.at[to],
            recv_sem=receive.at[spot],
            device_id={"dev": to},
            device_id_type=MESH,
        )

    def rotations(o, landing=None):
        return transfer(rot_ref, rrot, rot_send, rot_recv, o, landing)

    def messages(o, landing=None):
        return transfer(msg, recv, msg_send, msg_recv, o, landing)

    each(peers - 1, lambda o: rotations(o).start())
    rrot[me] = rot_ref[me]

    for copy in weights:
        copy.wait()
    exchange.wait()

    def mix(block):
        for pair in range((FRAME + 1) // 2):
            there = other[block, :, pair * LANES : (pair + 1) * LANES].astype(jnp.float32)
            for slot, value in ((2 * pair, there), (2 * pair + 1, None)):
                if slot < FRAME:
                    value = pltpu.roll(there, HALF, 1) if value is None else value
                    cols = slice(slot * LANES, (slot + 1) * LANES)
                    lhs[:, cols] = jnp.where(mine, own[block, :, cols], value).astype(jnp.bfloat16)
        nt = (((1,), (1,)), ((), ()))
        y_scr[:, 0 : 7 * HALF] = lax.dot_general(
            lhs[:, 0 : 7 * LANES], w0[...], nt, preferred_element_type=jnp.float32
        )
        for start, count, spots, ref, dims in (
            (7, 6, (512, 896), w1, (((1,), (0,)), ((), ()))),
            (19, 5, (1280, 1664), w2, nt),
        ):
            rows = jnp.concatenate(
                [
                    lhs[:, start * LANES : (start + count) * LANES],
                    lhs[:, (start + count) * LANES : (start + 2 * count) * LANES],
                ],
                axis=0,
            )
            real = lax.dot_general(rows, ref[0], dims, preferred_element_type=jnp.float32)
            imag = lax.dot_general(rows, ref[1], dims, preferred_element_type=jnp.float32)
            width = count * HALF
            y_scr[:, spots[0] : spots[0] + width] = real[:BLOCK] - imag[BLOCK:]
            y_scr[:, spots[1] : spots[1] + width] = imag[:BLOCK] + real[BLOCK:]
        for index in range(group):
            msg[block * group + index] = y_scr[index * slots : (index + 1) * slots, :].astype(
                jnp.bfloat16
            )

    each(blocks, mix)
    each(peers - 1, lambda o: messages(o).start())
    recv[me] = msg[me]

    def wait_rotation(o):
        rotations(o, peer(o + 1)).wait_recv()

    def wait_message(o):
        messages(o, peer(o + 1)).wait_recv()

    each(peers - 1, wait_rotation)

    def prepare(block):
        tables = load_rotation(rrot, block * group)
        for number, (slot, tile, first, second) in enumerate(TERMS):
            mult[number] = multiplier(tables, first, second)

    def collect(block, add):
        for index in range(group):
            f_scr[index * slots : (index + 1) * slots, :] = recv[block * group + index].astype(
                jnp.float32
            )
        doubled = {}
        for slot in range(FRAME):
            tile, side = message_place(slot)
            value = f_scr[:, tile * LANES : (tile + 1) * LANES]
            turned = pltpu.roll(value, HALF, 1)
            doubled[slot] = (
                jnp.where(low_half, value, turned) if side == 0 else jnp.where(low_half, turned, value)
            )
        sums = [None] * TILES
        for number, (slot, tile, first, second) in enumerate(TERMS):
            part = mult[number] * doubled[slot]
            sums[tile] = part if sums[tile] is None else sums[tile] + part
        for tile in range(TILES):
            back[:, tile * LANES : (tile + 1) * LANES] = sums[tile].astype(jnp.bfloat16)
        hot = (
            lax.broadcasted_iota(jnp.int32, (nodes, BLOCK), 0) == dst_ref[pl.ds(block, 1), :]
        ).astype(jnp.bfloat16)
        value = jnp.dot(hot, back[...], preferred_element_type=jnp.float32)
        total[...] = total[...] + value if add else value

    if blocks == 1:
        prepare(0)
        each(peers - 1, wait_message)
        collect(0, False)
    else:
        each(peers - 1, wait_message)
        total[...] = jnp.zeros_like(total)

        def one(block, carry):
            prepare(block)
            collect(block, True)
            return carry

        lax.fori_loop(0, blocks, one, 0)

    partial = None
    for tile in range(TILES):
        value = total[:, tile * LANES : (tile + 1) * LANES]
        partial = value * value if partial is None else partial + value * value
    sq[...] = partial
    share = pltpu.make_async_remote_copy(
        src_ref=sq,
        dst_ref=sq_other,
        send_sem=qsem.at[0],
        recv_sem=qsem.at[1],
        device_id=partner,
        device_id_type=MESH,
    )
    share.start()
    each(peers - 1, lambda o: rotations(o).wait_send())
    each(peers - 1, lambda o: messages(o).wait_send())
    share.wait()
    mean_sq = jnp.sum(sq[...] + sq_other[...], axis=1, keepdims=True) / (2 * flat)
    scale = lax.rsqrt(mean_sq + 1e-06)
    for start in range(0, flat, LANES):
        cols = slice(start, min(start + LANES, flat))
        normed = total[:, cols] * scale
        out_ref[:, cols] = (
            x_ref[:, cols].astype(jnp.float32) + gain_ref[:, cols] * normed
        ).astype(jnp.bfloat16)


def shards(node_features, src_node, dst_node, counts, rotation, w_zero, w_one, w_two, norm_gain):
    nodes, _, flat = node_features.shape
    peers, slots = src_node.shape[1:]
    edges = peers * slots
    blocks = edges // BLOCK
    x = node_features.reshape(nodes, flat)
    live = jnp.arange(slots)[None, :] < counts.reshape(peers)[:, None]
    src = jnp.where(live, src_node.reshape(peers, slots), -1).reshape(edges, 1)
    dst = dst_node.reshape(blocks, BLOCK)
    rot = rotation.reshape(peers, slots, ROT)
    w0 = w_zero.reshape(w_zero.shape[0], -1).T
    w1 = w_one.reshape(2, w_one.shape[1], -1)
    w2 = w_two.reshape(2, w_two.shape[1], -1).swapaxes(1, 2)
    vmem = pl.BlockSpec(memory_space=pltpu.VMEM)
    hbm = pl.BlockSpec(memory_space=pl.ANY)
    f32, bf16 = jnp.float32, jnp.bfloat16
    dma = pltpu.SemaphoreType.DMA
    pairs = (FRAME + 1) // 2
    out = pl.pallas_call(
        functools.partial(kernel, peers, slots),
        out_shape=jax.ShapeDtypeStruct((nodes, flat), bf16),
        in_specs=[vmem] * 5 + [hbm] * 3,
        out_specs=vmem,
        scratch_shapes=[
            pltpu.VMEM(w0.shape, bf16),
            pltpu.VMEM(w1.shape, bf16),
            pltpu.VMEM(w2.shape, bf16),
            pltpu.VMEM((BLOCK, LANES), f32),
            pltpu.VMEM((BLOCK, LANES), f32),
            pltpu.VMEM((BLOCK, WIDE), f32),
            pltpu.VMEM((blocks, BLOCK, FRAME * LANES), f32),
            pltpu.VMEM((blocks, BLOCK, pairs * LANES), bf16),
            pltpu.VMEM((blocks, BLOCK, pairs * LANES), bf16),
            pltpu.VMEM((BLOCK, FRAME * LANES), bf16),
            pltpu.VMEM((BLOCK, MESSAGE), f32),
            pltpu.VMEM((peers, slots, MESSAGE), bf16),
            pltpu.VMEM((peers, slots, MESSAGE), bf16),
            pltpu.VMEM((peers, slots, ROT), bf16),
            pltpu.VMEM((len(TERMS), BLOCK, LANES), f32),
            pltpu.VMEM((BLOCK, MESSAGE), f32),
            pltpu.VMEM((BLOCK, WIDE), bf16),
            pltpu.VMEM((nodes, WIDE), f32),
            pltpu.VMEM((nodes, LANES), f32),
            pltpu.VMEM((nodes, LANES), f32),
            dma((3,)),
            dma((2,)),
            dma((peers,)),
            dma((peers,)),
            dma((peers,)),
            dma((peers,)),
            dma((2,)),
        ],
        compiler_params=pltpu.CompilerParams(
            collective_id=0, has_side_effects=True, vmem_limit_bytes=40 * 1024 * 1024
        ),
    )(x, src, dst, rot, norm_gain, w0, w1, w2)
    return out.reshape(nodes, 1, flat)


def solution(mesh):
    return jax.shard_map(
        shards,
        mesh=mesh,
        in_specs=(
            P("dev", "rep", None),
            P("dev", None, None),
            P("dev", None, None),
            P("dev", None),
            P("dev", None, None, None),
            P(None, "rep", None),
            P(None, None, "rep", None),
            P(None, None, "rep", None),
            P("rep", None),
        ),
        out_specs=P("dev", "rep", None),
        check_vma=False,
    )
```

time: 44.9 us -> 24.2 us (0.54)
  Pallas kernels: 0 us -> 14.6 us
  waiting for transfers between devices: 8.86 us -> 0 us
  starting transfers between devices: 8.22 us -> 0 us
  blocking collectives: 5.19 us -> 0 us
  other arithmetic: 5.73 us -> 0.74 us
  local copies, waits for them, and re-layouts: 13.2 us -> 8.48 us
  matrix products: 2.61 us -> 0 us
  between operations: 0.73 us -> 0.03 us
    pallas_call x0 -> x1, Pallas kernels: none -> 14.6 us  [shards(): pl.pallas_call(functools.partial(kernel, peers, slots), out_shape=jax.Sha...]
    all_to_all x1 -> x0, waiting for transfers between devices: 8.86 us -> none  [shards(): lax.all_to_all(for_sending(outgoing), 'dev', split_axis=0, concat_axis=0,...]
    all_to_all x1 -> x0, starting transfers between devices: 8.22 us -> none  [shards(): lax.all_to_all(for_sending(outgoing), 'dev', split_axis=0, concat_axis=0,...]
    reshape x9 -> x2, local copies, waits for them, and re-layouts: 7.77 us -> 0.16 us  [the longest x1 0.09 us: shards(): dst = dst_node.reshape(blocks, BLOCK)]
    unnamed x56 -> x15, local copies, waits for them, and re-layouts: 3.15 us -> 8.24 us
    reduce_sum x12 -> x0, other arithmetic: 2.79 us -> none  [the longest x6 1.39 us: unframe(): parts.append(jnp.sum(matrix[:, :, :, None] * chosen[:, :, None, :], axis=1))]
    all_gather x1 -> x0, blocking collectives: 2.72 us -> none  [shards(): both = lax.all_gather(node_features, 'rep', axis=1, tiled=True)]
    dot_general x10 -> x0, matrix products: 2.61 us -> none  [the longest x1 0.49 us: mix_orders(): jnp.dot(flat_zero, zero_mat, preferred_element_type=jnp.float32)]
  transfers between devices with their start and end apart: 1 -> 0, of which waited for: 1 -> 0; matrix products, arithmetic and copies ran while one was open for 0% -> 0% of each run, Pallas kernels for 0% -> 0%
where the time goes in v1:
time: 24.2 us; the launch traced here: 23.8 us
  Pallas kernels  14.6 us (60%)
  local copies, waits for them, and re-layouts  8.48 us (35%)
  other arithmetic  0.74 us (3%)
    pallas_call x1, Pallas kernels, shards(): pl.pallas_call(functools.partial(kernel, peers, slots), out_shape=jax.Sha...  14.6 us
    unnamed x15, local copies, waits for them, and re-layouts  8.24 us
    lt x1, other arithmetic, shards(): live = jnp.arange(slots)[None, :] < counts.reshape(peers)[:, None]  0.73 us

profile of v1, /device:TPU:0, one launch (start us, length us, event | category | flops | bytes accessed | tf_op | source)
XLA Modules:
  0.0 23.8 jit_solution(6118831406837341520)
XLA Ops:
  0.0 0.7 %iota_compare_fusion = pred[16,2]{1,0:T(8,128)(4,1)S(1)} fusion(s32[16]{0:T(128)} %bitcast.17), kind=kLoop, calls=%fused_computation.1 | loop fusion | flops 32 | bytes 96 | tf_op jit(solution)/shard_map/lt | solution.py:347
  0.7 0.1 lt.30
  0.8 0.8 %copy.14 = s32[1,16,2]{2,1,0:T(8,128)S(1)} copy(s32[1,16,2]{1,2,0:T(2,128)} %param.10) | data formatting | bytes 256 | tf_op args[1]
  1.6 0.1 reshape.66
  1.6 0.8 %copy.17 = s32[1,16,2]{2,1,0:T(8,128)S(1)} copy(s32[1,16,2]{1,2,0:T(2,128)} %param.11) | data formatting | bytes 256 | tf_op args[2]
  2.4 0.1 reshape.60.dst_ref
  2.5 0.0 copy-start
  2.5 1.3 %copy-done = bf16[2,768,1,384]{3,1,2,0:T(8,128)(2,1)S(1)} copy-done((bf16[2,768,1,384]{3,1,2,0:T(8,128)(2,1)S(1)}, bf16[2,768,1,384]{3,1,2,0:T(8,128)(2,1)}, u32[]{:S(2)}) %copy-start) | copy-done | bytes 1179672
  3.8 0.0 copy-start.1
  3.8 1.1 %copy-done.1 = bf16[2,640,1,320]{1,3,2,0:T(8,128)(2,1)S(1)} copy-done((bf16[2,640,1,320]{1,3,2,0:T(8,128)(2,1)S(1)}, bf16[2,640,1,320]{1,3,2,0:T(8,128)(2,1)}, u32[]{:S(2)}) %copy-start.1) | copy-done | bytes 819224
  4.9 0.0 copy-start.2
  4.9 1.1 %copy-done.2 = bf16[896,1,448]{0,2,1:T(8,128)(2,1)S(1)} copy-done((bf16[896,1,448]{0,2,1:T(8,128)(2,1)S(1)}, bf16[896,1,448]{0,2,1:T(8,128)(2,1)}, u32[]{:S(2)}) %copy-start.2) | copy-done | bytes 802840
  6.1 0.0 copy-start.3
  6.1 1.0 %copy-done.3 = bf16[64,1,3136]{2,0,1:T(8,128)(2,1)S(1)} copy-done((bf16[64,1,3136]{2,0,1:T(8,128)(2,1)S(1)}, bf16[64,1,3136]{2,0,1:T(8,128)(2,1)}, u32[]{:S(2)}) %copy-start.3) | copy-done | bytes 401432
  7.1 0.0 copy-start.4
  7.1 0.7 %copy-done.4 = bf16[1,16,2,235]{3,2,1,0:T(2,128)(2,1)S(1)} copy-done((bf16[1,16,2,235]{3,2,1,0:T(2,128)(2,1)S(1)}, bf16[1,16,2,235]{3,2,1,0:T(2,128)(2,1)}, u32[]{:S(2)}) %copy-start.4) | copy-done | bytes 15064
  7.8 0.0 copy-start.5
  7.8 0.7 %copy-done.5 = f32[1,3136]{1,0:T(1,128)S(1)} copy-done((f32[1,3136]{1,0:T(1,128)S(1)}, f32[1,3136]{1,0:T(1,128)}, u32[]{:S(2)}) %copy-start.5) | copy-done | bytes 12568
  8.5 14.6 %shard_map.91 = bf16[64,3136]{1,0:T(8,128)(2,1)S(1)} custom-call(bf16[64,3136]{1,0:T(8,128)(2,1)S(1)} %bitcast.15, s32[32,1]{1,0:T(8,128)S(1)} %broadcast_select_fusion.src_ref, s32[1,32]{1,0:T(1,128)S(1)} %reshape.60.dst_ref, bf16[16,2,235]{2,1,0:T(2,128)(2,1)S(1)} %bitcast.16, f32[1,3136]{1,0:T(1,128)S(1)} %copy-done.5, bf16[448,896]{1,0:T(8,128)(2,1)S(1)} %bitcast.14, ...), custom_call_target="tpu_custom_call" | custom-call | tf_op jit(solution)/shard_map/pallas_call | solution.py:359
  23.1 0.8 %copy.19 = bf16[64,1,3136]{2,0,1:T(8,128)(2,1)} copy(bf16[64,1,3136]{2,0,1:T(8,128)(2,1)S(1)} %bitcast.11) | data formatting | bytes 802816
  (1 shorter events, 0.0 us)
Async XLA Ops:
  2.5 1.3 %copy-start = (bf16[2,768,1,384]{3,1,2,0:T(8,128)(2,1)S(1)}, bf16[2,768,1,384]{3,1,2,0:T(8,128)(2,1)}, u32[]{:S(2)}) copy-start(bf16[2,768,1,384]{3,1,2,0:T(8,128)(2,1)} %param.15) | copy-start | bytes 3538948
  3.8 1.1 %copy-start.1 = (bf16[2,640,1,320]{1,3,2,0:T(8,128)(2,1)S(1)}, bf16[2,640,1,320]{1,3,2,0:T(8,128)(2,1)}, u32[]{:S(2)}) copy-start(bf16[2,640,1,320]{1,3,2,0:T(8,128)(2,1)} %param.16) | copy-start | bytes 2457604
  4.9 1.1 %copy-start.2 = (bf16[896,1,448]{0,2,1:T(8,128)(2,1)S(1)}, bf16[896,1,448]{0,2,1:T(8,128)(2,1)}, u32[]{:S(2)}) copy-start(bf16[896,1,448]{0,2,1:T(8,128)(2,1)} %param.14) | copy-start | bytes 2408452
  6.1 1.0 %copy-start.3 = (bf16[64,1,3136]{2,0,1:T(8,128)(2,1)S(1)}, bf16[64,1,3136]{2,0,1:T(8,128)(2,1)}, u32[]{:S(2)}) copy-start(bf16[64,1,3136]{2,0,1:T(8,128)(2,1)} %param.9) | copy-start | bytes 1204228
  7.1 0.7 %copy-start.4 = (bf16[1,16,2,235]{3,2,1,0:T(2,128)(2,1)S(1)}, bf16[1,16,2,235]{3,2,1,0:T(2,128)(2,1)}, u32[]{:S(2)}) copy-start(bf16[1,16,2,235]{3,2,1,0:T(2,128)(2,1)} %param.13) | copy-start | bytes 45124
  7.8 0.7 %copy-start.5 = (f32[1,3136]{1,0:T(1,128)S(1)}, f32[1,3136]{1,0:T(1,128)}, u32[]{:S(2)}) copy-start(f32[1,3136]{1,0:T(1,128)} %gain_ref.1) | copy-start | bytes 37636

commit v2 on v1

--- a/solution.py
+++ b/solution.py
@@ -17,6 +17,7 @@
 WIDE = TILES * LANES
 GROUPS = ((0, 7, 0), (7, 6, 512), (13, 6, 896), (19, 5, 1280), (24, 5, 1664))
 MESSAGE = 2048
+VMEM_LIMIT = 67043328
 BLOCK = 32
 MESH = pl.DeviceIdType.MESH
 
@@ -74,15 +75,22 @@
 def kernel(
     peers,
     slots,
-    x_ref,
-    src_ref,
-    dst_ref,
-    rot_ref,
-    gain_ref,
+    x_hbm,
+    rot_hbm,
+    src_hbm,
+    cnt_hbm,
+    dst_hbm,
+    gain_hbm,
     w0_hbm,
     w1_hbm,
     w2_hbm,
     out_ref,
+    x_ref,
+    rot_ref,
+    src_ref,
+    cnt_ref,
+    dst_ref,
+    gain_ref,
     w0,
     w1,
     w2,
@@ -122,10 +130,24 @@
     def peer(offset):
         return lax.rem(me + offset, peers)
 
-    weights = [
+    loads = [
         pltpu.make_async_copy(src, dst, wsem.at[index])
-        for index, (src, dst) in enumerate(((w0_hbm, w0), (w1_hbm, w1), (w2_hbm, w2)))
+        for index, (src, dst) in enumerate(
+            (
+                (x_hbm, x_ref),
+                (rot_hbm, rot_ref),
+                (src_hbm, src_ref),
+                (cnt_hbm, cnt_ref),
+                (dst_hbm, dst_ref),
+                (gain_hbm, gain_ref),
+                (w0_hbm, w0),
+                (w1_hbm, w1),
+                (w2_hbm, w2),
+            )
+        )
     ]
+    for copy in loads:
+        copy.start()
     barrier = pltpu.get_barrier_semaphore()
     pl.semaphore_signal(barrier, inc=1, device_id=partner, device_id_type=MESH)
     each(
@@ -134,8 +156,6 @@
             barrier, inc=1, device_id={"dev": peer(o + 1)}, device_id_type=MESH
         ),
     )
-    for copy in weights:
-        copy.start()
 
     lane = lax.broadcasted_iota(jnp.int32, (BLOCK, LANES), 1)
     low_half = lane < HALF
@@ -145,6 +165,31 @@
     xg[:, (TILES - 1) * LANES :] = jnp.zeros((BLOCK, LANES), jnp.float32)
     low_scr[...] = jnp.zeros_like(low_scr)
     high_scr[...] = jnp.zeros_like(high_scr)
+
+    def column(rows):
+        row = lax.broadcasted_iota(jnp.int32, (BLOCK, group), 0)
+        spot = lax.broadcasted_iota(jnp.int32, (BLOCK, group), 1)
+        chosen = jnp.zeros((BLOCK, group), jnp.float32)
+        for index in range(slots):
+            chosen = jnp.where(row == spot * slots + index, rows[index], chosen)
+        return jnp.sum(chosen, axis=1, keepdims=True)
+
+    def sources(block):
+        count = cnt_ref[block]
+        value = src_ref[block]
+        return column(
+            [
+                jnp.where(count > index, value[index : index + 1], -1).astype(jnp.float32)
+                for index in range(slots)
+            ]
+        )
+
+    def targets(block):
+        value = dst_ref[block].astype(jnp.float32)
+        down = column([value[index : index + 1] for index in range(slots)])
+        row = lax.broadcasted_iota(jnp.int32, (BLOCK, BLOCK), 0)
+        spot = lax.broadcasted_iota(jnp.int32, (BLOCK, BLOCK), 1)
+        return jnp.sum(jnp.where(row == spot, down, 0.0), axis=0, keepdims=True)
 
     def load_rotation(ref, start):
         for index in range(group):
@@ -163,9 +208,8 @@
 
     def turn(block):
         tables = load_rotation(rot_ref, block * group)
-        rows = pl.multiple_of(block * BLOCK, BLOCK)
         hot = (
-            lax.broadcasted_iota(jnp.int32, (BLOCK, nodes), 1) == src_ref[pl.ds(rows, BLOCK), :]
+            lax.broadcasted_iota(jnp.int32, (BLOCK, nodes), 1).astype(jnp.float32) == sources(block)
         ).astype(jnp.bfloat16)
         xg[:, 0:flat] = jnp.dot(hot, x_ref[...], preferred_element_type=jnp.float32)
         sums = [None] * FRAME
@@ -182,6 +226,8 @@
                 mine, first, second
             ).astype(jnp.bfloat16)
 
+    for copy in loads[:4]:
+        copy.wait()
     each(blocks, turn)
 
     pl.semaphore_wait(barrier, peers)
@@ -217,7 +263,7 @@
     each(peers - 1, lambda o: rotations(o).start())
     rrot[me] = rot_ref[me]
 
-    for copy in weights:
+    for copy in loads[4:]:
         copy.wait()
     exchange.wait()
 
@@ -291,7 +337,7 @@
         for tile in range(TILES):
             back[:, tile * LANES : (tile + 1) * LANES] = sums[tile].astype(jnp.bfloat16)
         hot = (
-            lax.broadcasted_iota(jnp.int32, (nodes, BLOCK), 0) == dst_ref[pl.ds(block, 1), :]
+            lax.broadcasted_iota(jnp.int32, (nodes, BLOCK), 0).astype(jnp.float32) == targets(block)
         ).astype(jnp.bfloat16)
         value = jnp.dot(hot, back[...], preferred_element_type=jnp.float32)
         total[...] = total[...] + value if add else value
@@ -344,9 +390,10 @@
     edges = peers * slots
     blocks = edges // BLOCK
     x = node_features.reshape(nodes, flat)
-    live = jnp.arange(slots)[None, :] < counts.reshape(peers)[:, None]
-    src = jnp.where(live, src_node.reshape(peers, slots), -1).reshape(edges, 1)
-    dst = dst_node.reshape(blocks, BLOCK)
+    group = peers // blocks
+    src = src_node.reshape(blocks, group, slots).swapaxes(1, 2)
+    dst = dst_node.reshape(blocks, group, slots).swapaxes(1, 2)
+    cnt = counts.reshape(blocks, 1, group)
     rot = rotation.reshape(peers, slots, ROT)
     w0 = w_zero.reshape(w_zero.shape[0], -1).T
     w1 = w_one.reshape(2, w_one.shape[1], -1)
@@ -359,9 +406,15 @@
     out = pl.pallas_call(
         functools.partial(kernel, peers, slots),
         out_shape=jax.ShapeDtypeStruct((nodes, flat), bf16),
-        in_specs=[vmem] * 5 + [hbm] * 3,
+        in_specs=[hbm] * 9,
         out_specs=vmem,
         scratch_shapes=[
+            pltpu.VMEM(x.shape, bf16),
+            pltpu.VMEM(rot.shape, bf16),
+            pltpu.VMEM(src.shape, jnp.int32),
+            pltpu.VMEM(cnt.shape, jnp.int32),
+            pltpu.VMEM(dst.shape, jnp.int32),
+            pltpu.VMEM(norm_gain.shape, f32),
             pltpu.VMEM(w0.shape, bf16),
             pltpu.VMEM(w1.shape, bf16),
             pltpu.VMEM(w2.shape, bf16),
@@ -382,7 +435,7 @@
             pltpu.VMEM((nodes, WIDE), f32),
             pltpu.VMEM((nodes, LANES), f32),
             pltpu.VMEM((nodes, LANES), f32),
-            dma((3,)),
+            dma((9,)),
             dma((2,)),
             dma((peers,)),
             dma((peers,)),
@@ -391,9 +444,9 @@
             dma((2,)),
         ],
         compiler_params=pltpu.CompilerParams(
-            collective_id=0, has_side_effects=True, vmem_limit_bytes=40 * 1024 * 1024
+            collective_id=0, has_side_effects=True, vmem_limit_bytes=VMEM_LIMIT
         ),
-    )(x, src, dst, rot, norm_gain, w0, w1, w2)
+    )(x, rot, src, cnt, dst, norm_gain, w0, w1, w2)
     return out.reshape(nodes, 1, flat)
 
 

time: 24.2 us -> 17.9 us (0.74)
  local copies, waits for them, and re-layouts: 8.48 us -> 1.78 us
  Pallas kernels: 14.6 us -> 15.9 us
  other arithmetic: 0.74 us -> 0 us
    unnamed x15 -> x1, local copies, waits for them, and re-layouts: 8.24 us -> 1.78 us
    pallas_call x1, Pallas kernels: 14.6 us -> 15.9 us  [shards(): pl.pallas_call(functools.partial(kernel, peers, slots), out_shape=jax.Sha...]
    lt x1 -> x0, other arithmetic: 0.73 us -> none  [shards(): live = jnp.arange(slots)[None, :] < counts.reshape(peers)[:, None]]
where the time goes in v2:
time: 17.9 us; the launch traced here: 17.7 us
  Pallas kernels  15.9 us (89%)
  local copies, waits for them, and re-layouts  1.78 us (10%)
    pallas_call x1, Pallas kernels, shards(): pl.pallas_call(functools.partial(kernel, peers, slots), out_shape=jax.Sha...  15.9 us
    unnamed x1, local copies, waits for them, and re-layouts  1.78 us

profile of v2, /device:TPU:0, one launch (start us, length us, event | category | flops | bytes accessed | tf_op | source)
XLA Modules:
  0.0 17.7 jit_solution(3610010339749142915)
XLA Ops:
  0.0 15.9 %shard_map.91 = bf16[64,3136]{1,0:T(8,128)(2,1)} custom-call(bf16[64,3136]{1,0:T(8,128)(2,1)} %bitcast.17, bf16[16,2,235]{2,1,0:T(2,128)(2,1)} %bitcast.18, s32[1,2,16]{2,1,0:T(2,128)} %bitcast.19, s32[1,1,16]{2,1,0:T(1,128)} %bitcast.21, s32[1,2,16]{2,1,0:T(2,128)} %bitcast.20, f32[1,3136]{1,0:T(1,128)} %gain_hbm.1, bf16[448,896]{1,0:T(8,128)(2,1)} %bitcast.16, ...), custom_call_target="tpu_custom_call" | custom-call | tf_op jit(solution)/shard_map/pallas_call | solution.py:406
  15.9 1.8 %copy.11 = bf16[64,1,3136]{2,0,1:T(8,128)(2,1)} copy(bf16[64,1,3136]{2,0,1:T(8,128)(2,1)} %bitcast.13) | data formatting | bytes 802816

commit v3 on v2

--- a/solution.py
+++ b/solution.py
@@ -15,9 +15,8 @@
 WINDOW = 120
 TILES = (COEFFS + 1) // 2
 WIDE = TILES * LANES
-GROUPS = ((0, 7, 0), (7, 6, 512), (13, 6, 896), (19, 5, 1280), (24, 5, 1664))
-MESSAGE = 2048
-VMEM_LIMIT = 67043328
+MESSAGE = (FRAME + 1) // 2 * LANES
+VMEM_LIMIT = 40 * 1024 * 1024
 BLOCK = 32
 MESH = pl.DeviceIdType.MESH
 
@@ -57,11 +56,19 @@
 
 
 def message_place(slot):
-    for first, count, base in GROUPS:
-        if first <= slot < first + count:
-            lane = base + (slot - first) * HALF
-            return lane // LANES, (lane % LANES) // HALF
-    raise ValueError
+    return slot // 2, slot % 2
+
+
+def far_first(count):
+    return sorted(range(1, count), key=lambda offset: -min(offset, count - offset))
+
+
+def each_peer(count, func):
+    if count <= 17:
+        for offset in far_first(count):
+            func(offset - 1)
+    else:
+        each(count - 1, func)
 
 
 def each(count, func):
@@ -260,7 +267,7 @@
     def messages(o, landing=None):
         return transfer(msg, recv, msg_send, msg_recv, o, landing)
 
-    each(peers - 1, lambda o: rotations(o).start())
+    each_peer(peers, lambda o: rotations(o).start())
     rrot[me] = rot_ref[me]
 
     for copy in loads[4:]:
@@ -279,9 +286,9 @@
         y_scr[:, 0 : 7 * HALF] = lax.dot_general(
             lhs[:, 0 : 7 * LANES], w0[...], nt, preferred_element_type=jnp.float32
         )
-        for start, count, spots, ref, dims in (
-            (7, 6, (512, 896), w1, (((1,), (0,)), ((), ()))),
-            (19, 5, (1280, 1664), w2, nt),
+        for start, count, ref, dims in (
+            (7, 6, w1, (((1,), (0,)), ((), ()))),
+            (19, 5, w2, nt),
         ):
             rows = jnp.concatenate(
                 [
@@ -293,15 +300,17 @@
             real = lax.dot_general(rows, ref[0], dims, preferred_element_type=jnp.float32)
             imag = lax.dot_general(rows, ref[1], dims, preferred_element_type=jnp.float32)
             width = count * HALF
-            y_scr[:, spots[0] : spots[0] + width] = real[:BLOCK] - imag[BLOCK:]
-            y_scr[:, spots[1] : spots[1] + width] = imag[:BLOCK] + real[BLOCK:]
+            plus = start * HALF
+            minus = plus + width
+            y_scr[:, plus : plus + width] = real[:BLOCK] - imag[BLOCK:]
+            y_scr[:, minus : minus + width] = imag[:BLOCK] + real[BLOCK:]
         for index in range(group):
             msg[block * group + index] = y_scr[index * slots : (index + 1) * slots, :].astype(
                 jnp.bfloat16
             )
 
     each(blocks, mix)
-    each(peers - 1, lambda o: messages(o).start())
+    each_peer(peers, lambda o: messages(o).start())
     recv[me] = msg[me]
 
     def wait_rotation(o):
@@ -399,10 +408,11 @@
     w1 = w_one.reshape(2, w_one.shape[1], -1)
     w2 = w_two.reshape(2, w_two.shape[1], -1).swapaxes(1, 2)
     vmem = pl.BlockSpec(memory_space=pltpu.VMEM)
-    hbm = pl.BlockSpec(memory_space=pl.ANY)
+    hbm = pl.BlockSpec(memory_space=pltpu.HBM)
     f32, bf16 = jnp.float32, jnp.bfloat16
     dma = pltpu.SemaphoreType.DMA
     pairs = (FRAME + 1) // 2
+    operands = (x, rot, src, cnt, dst, norm_gain, w0, w1, w2)
     out = pl.pallas_call(
         functools.partial(kernel, peers, slots),
         out_shape=jax.ShapeDtypeStruct((nodes, flat), bf16),
@@ -446,7 +456,7 @@
         compiler_params=pltpu.CompilerParams(
             collective_id=0, has_side_effects=True, vmem_limit_bytes=VMEM_LIMIT
         ),
-    )(x, rot, src, cnt, dst, norm_gain, w0, w1, w2)
+    )(*(pltpu.with_memory_space_constraint(operand, pltpu.HBM) for operand in operands))
     return out.reshape(nodes, 1, flat)
 
 

time: 17.9 us -> 17.5 us (0.978)
  local copies, waits for them, and re-layouts: 1.78 us -> 0.75 us
  Pallas kernels: 15.9 us -> 16.6 us
    unnamed x1, local copies, waits for them, and re-layouts: 1.78 us -> 0.75 us
    pallas_call x1, Pallas kernels: 15.9 us -> 16.6 us  [shards(): pl.pallas_call(functools.partial(kernel, peers, slots), out_shape=jax.Sha...]
where the time goes in v3:
time: 17.5 us; the launch traced here: 17.4 us
  Pallas kernels  16.6 us (95%)
  local copies, waits for them, and re-layouts  0.75 us (4%)
    pallas_call x1, Pallas kernels, shards(): pl.pallas_call(functools.partial(kernel, peers, slots), out_shape=jax.Sha...  16.6 us
    unnamed x1, local copies, waits for them, and re-layouts  0.75 us

profile of v3, /device:TPU:0, one launch (start us, length us, event | category | flops | bytes accessed | tf_op | source)
XLA Modules:
  0.0 17.4 jit_solution(2897565618643018449)
XLA Ops:
  0.0 16.6 %shard_map.91 = bf16[64,3136]{1,0:T(8,128)(2,1)S(1)} custom-call(bf16[64,3136]{1,0:T(8,128)(2,1)} %bitcast.17, bf16[16,2,235]{2,1,0:T(2,128)(2,1)} %bitcast.18, s32[1,2,16]{2,1,0:T(2,128)} %bitcast.19, s32[1,1,16]{2,1,0:T(1,128)} %bitcast.21, s32[1,2,16]{2,1,0:T(2,128)} %bitcast.20, f32[1,3136]{1,0:T(1,128)} %gain_hbm.1, bf16[448,896]{1,0:T(8,128)(2,1)} %bitcast.16, ...), custom_call_target="tpu_custom_call" | custom-call | tf_op jit(solution)/shard_map/pallas_call | solution.py:416
  16.6 0.8 %copy.11 = bf16[64,1,3136]{2,0,1:T(8,128)(2,1)} copy(bf16[64,1,3136]{2,0,1:T(8,128)(2,1)S(1)} %bitcast.13) | data formatting | bytes 802816

commit v4 on v3

--- a/solution.py
+++ b/solution.py
@@ -61,6 +61,11 @@
 
 def far_first(count):
     return sorted(range(1, count), key=lambda offset: -min(offset, count - offset))
+
+
+def cube_bits(count):
+    bits = [1 << place for place in range(count.bit_length() - 1)]
+    return bits if count == 1 << len(bits) else []
 
 
 def each_peer(count, func):
@@ -125,6 +130,7 @@
     msg_send,
     msg_recv,
     qsem,
+    ready,
 ):
     me = lax.axis_index("dev")
     half = lax.axis_index("rep")
@@ -157,12 +163,20 @@
         copy.start()
     barrier = pltpu.get_barrier_semaphore()
     pl.semaphore_signal(barrier, inc=1, device_id=partner, device_id_type=MESH)
-    each(
-        peers - 1,
-        lambda o: pl.semaphore_signal(
-            barrier, inc=1, device_id={"dev": peer(o + 1)}, device_id_type=MESH
-        ),
-    )
+    bits = cube_bits(peers)
+
+    def across(bit):
+        return me + bit - 2 * bit * lax.rem(me // bit, 2)
+
+    for bit in bits:
+        pl.semaphore_signal(barrier, inc=1, device_id={"dev": across(bit)}, device_id_type=MESH)
+    if not bits:
+        each(
+            peers - 1,
+            lambda o: pl.semaphore_signal(
+                barrier, inc=1, device_id={"dev": peer(o + 1)}, device_id_type=MESH
+            ),
+        )
 
     lane = lax.broadcasted_iota(jnp.int32, (BLOCK, LANES), 1)
     low_half = lane < HALF
@@ -237,7 +251,7 @@
         copy.wait()
     each(blocks, turn)
 
-    pl.semaphore_wait(barrier, peers)
+    pl.semaphore_wait(barrier, 1 + len(bits) if bits else peers)
 
     exchange = pltpu.make_async_remote_copy(
         src_ref=packed,
@@ -248,6 +262,22 @@
         device_id_type=MESH,
     )
     exchange.start()
+
+    stages = bits[:-1]
+
+    def tell(stage):
+        if stage < len(stages):
+            pl.semaphore_signal(
+                ready.at[stage],
+                inc=1,
+                device_id={"dev": across(stages[stage])},
+                device_id_type=MESH,
+            )
+
+    tell(0)
+    for stage in range(len(stages) - 1):
+        pl.semaphore_wait(ready.at[stage], 1)
+        tell(stage + 1)
 
     def transfer(source, target, send, receive, o, landing):
         to = peer(o + 1)
@@ -266,9 +296,6 @@
 
     def messages(o, landing=None):
         return transfer(msg, recv, msg_send, msg_recv, o, landing)
-
-    each_peer(peers, lambda o: rotations(o).start())
-    rrot[me] = rot_ref[me]
 
     for copy in loads[4:]:
         copy.wait()
@@ -310,7 +337,11 @@
             )
 
     each(blocks, mix)
+    if stages:
+        pl.semaphore_wait(ready.at[len(stages) - 1], 1)
+    each_peer(peers, lambda o: rotations(o).start())
     each_peer(peers, lambda o: messages(o).start())
+    rrot[me] = rot_ref[me]
     recv[me] = msg[me]
 
     def wait_rotation(o):
@@ -452,6 +483,7 @@
             dma((peers,)),
             dma((peers,)),
             dma((2,)),
+            pltpu.SemaphoreType.REGULAR((max(1, len(cube_bits(peers))),)),
         ],
         compiler_params=pltpu.CompilerParams(
             collective_id=0, has_side_effects=True, vmem_limit_bytes=VMEM_LIMIT

time: 17.5 us -> 17.8 us (1.017)
  Pallas kernels: 16.6 us -> 16.9 us
    pallas_call x1, Pallas kernels: 16.6 us -> 16.9 us  [shards(): pl.pallas_call(functools.partial(kernel, peers, slots), out_shape=jax.Sha...]
where the time goes in v4:
time: 17.8 us; the launch traced here: 17.7 us
  Pallas kernels  16.9 us (95%)
  local copies, waits for them, and re-layouts  0.75 us (4%)
    pallas_call x1, Pallas kernels, shards(): pl.pallas_call(functools.partial(kernel, peers, slots), out_shape=jax.Sha...  16.9 us
    unnamed x1, local copies, waits for them, and re-layouts  0.75 us

profile of v4, /device:TPU:0, one launch (start us, length us, event | category | flops | bytes accessed | tf_op | source)
XLA Modules:
  0.0 17.7 jit_solution(14490065087414721129)
XLA Ops:
  0.0 16.9 %shard_map.91 = bf16[64,3136]{1,0:T(8,128)(2,1)S(1)} custom-call(bf16[64,3136]{1,0:T(8,128)(2,1)} %bitcast.17, bf16[16,2,235]{2,1,0:T(2,128)(2,1)} %bitcast.18, s32[1,2,16]{2,1,0:T(2,128)} %bitcast.19, s32[1,1,16]{2,1,0:T(1,128)} %bitcast.21, s32[1,2,16]{2,1,0:T(2,128)} %bitcast.20, f32[1,3136]{1,0:T(1,128)} %gain_hbm.1, bf16[448,896]{1,0:T(8,128)(2,1)} %bitcast.16, ...), custom_call_target="tpu_custom_call" | custom-call | tf_op jit(solution)/shard_map/pallas_call | solution.py:447
  17.0 0.8 %copy.11 = bf16[64,1,3136]{2,0,1:T(8,128)(2,1)} copy(bf16[64,1,3136]{2,0,1:T(8,128)(2,1)S(1)} %bitcast.13) | data formatting | bytes 802816

commit v5 on v3

--- a/solution.py
+++ b/solution.py
@@ -11,6 +11,7 @@
 HALF = 64
 COEFFS = 49
 FRAME = 29
+CUT = 20
 ROT = 235
 WINDOW = 120
 TILES = (COEFFS + 1) // 2
@@ -213,20 +214,44 @@
         index = jnp.where(low_half, places[0], places[1])
         return jnp.take_along_axis(tables[which], index, axis=1, mode="promise_in_bounds")
 
+    middle = CUT // 2 * LANES
+    exchanges = [
+        pltpu.make_async_remote_copy(
+            src_ref=packed.at[:, :, cols],
+            dst_ref=other.at[:, :, cols],
+            send_sem=esem.at[2 * index],
+            recv_sem=esem.at[2 * index + 1],
+            device_id=partner,
+            device_id_type=MESH,
+        )
+        for index, cols in enumerate(
+            (pl.ds(0, middle), pl.ds(middle, (FRAME + 1) // 2 * LANES - middle))
+        )
+    ]
+
     def turn(block):
         tables = load_rotation(rot_ref, block * group)
         hot = (
             lax.broadcasted_iota(jnp.int32, (BLOCK, nodes), 1).astype(jnp.float32) == sources(block)
         ).astype(jnp.bfloat16)
         xg[:, 0:flat] = jnp.dot(hot, x_ref[...], preferred_element_type=jnp.float32)
+        rotate(block, tables, 0, CUT)
+        if blocks == 1:
+            pl.semaphore_wait(barrier, peers)
+            exchanges[0].start()
+        rotate(block, tables, CUT, FRAME)
+
+    def rotate(block, tables, begin, end):
         sums = [None] * FRAME
         for slot, tile, first, second in TERMS:
+            if not begin <= slot < end:
+                continue
             part = multiplier(tables, first, second) * xg[:, tile * LANES : (tile + 1) * LANES]
             sums[slot] = part if sums[slot] is None else sums[slot] + part
-        for slot in range(FRAME):
+        for slot in range(begin, end):
             sums[slot] = sums[slot] + pltpu.roll(sums[slot], HALF, 1)
             own[block, :, slot * LANES : (slot + 1) * LANES] = sums[slot]
-        for pair in range((FRAME + 1) // 2):
+        for pair in range(begin // 2, (end + 1) // 2):
             first = sums[2 * pair]
             second = sums[min(2 * pair + 1, FRAME - 1)]
             packed[block, :, pair * LANES : (pair + 1) * LANES] = jnp.where(
@@ -237,17 +262,10 @@
         copy.wait()
     each(blocks, turn)
 
-    pl.semaphore_wait(barrier, peers)
-
-    exchange = pltpu.make_async_remote_copy(
-        src_ref=packed,
-        dst_ref=other,
-        send_sem=esem.at[0],
-        recv_sem=esem.at[1],
-        device_id=partner,
-        device_id_type=MESH,
-    )
-    exchange.start()
+    if blocks > 1:
+        pl.semaphore_wait(barrier, peers)
+        exchanges[0].start()
+    exchanges[1].start()
 
     def transfer(source, target, send, receive, o, landing):
         to = peer(o + 1)
@@ -272,7 +290,8 @@
 
     for copy in loads[4:]:
         copy.wait()
-    exchange.wait()
+    for copy in exchanges:
+        copy.wait()
 
     def mix(block):
         for pair in range((FRAME + 1) // 2):
@@ -446,7 +465,7 @@
             pltpu.VMEM((nodes, LANES), f32),
             pltpu.VMEM((nodes, LANES), f32),
             dma((9,)),
-            dma((2,)),
+            dma((4,)),
             dma((peers,)),
             dma((peers,)),
             dma((peers,)),

time: 17.5 us -> 17.6 us (level)
  no operation moved by 1% of the time
where the time goes in v5:
time: 17.6 us; the launch traced here: 17.4 us
  Pallas kernels  16.7 us (95%)
  local copies, waits for them, and re-layouts  0.75 us (4%)
    pallas_call x1, Pallas kernels, shards(): pl.pallas_call(functools.partial(kernel, peers, slots), out_shape=jax.Sha...  16.7 us
    unnamed x1, local copies, waits for them, and re-layouts  0.75 us

profile of v5, /device:TPU:0, one launch (start us, length us, event | category | flops | bytes accessed | tf_op | source)
XLA Modules:
  0.0 17.4 jit_solution(9882291439148338556)
XLA Ops:
  0.0 16.7 %shard_map.91 = bf16[64,3136]{1,0:T(8,128)(2,1)S(1)} custom-call(bf16[64,3136]{1,0:T(8,128)(2,1)} %bitcast.17, bf16[16,2,235]{2,1,0:T(2,128)(2,1)} %bitcast.18, s32[1,2,16]{2,1,0:T(2,128)} %bitcast.19, s32[1,1,16]{2,1,0:T(1,128)} %bitcast.21, s32[1,2,16]{2,1,0:T(2,128)} %bitcast.20, f32[1,3136]{1,0:T(1,128)} %gain_hbm.1, bf16[448,896]{1,0:T(8,128)(2,1)} %bitcast.16, ...), custom_call_target="tpu_custom_call" | custom-call | tf_op jit(solution)/shard_map/pallas_call | solution.py:435
  16.7 0.8 %copy.11 = bf16[64,1,3136]{2,0,1:T(8,128)(2,1)} copy(bf16[64,1,3136]{2,0,1:T(8,128)(2,1)S(1)} %bitcast.13) | data formatting | bytes 802816
